TPU v7x, 32 devices: a whole 2x2x4 slice. The times are simulated.
32 devices in a mesh: node: 8 (over z, x), feat: 4 (over y, core).
Axes of the slice: x: 2, y: 2, z: 4, core: 2. Of those that a mesh axis runs over, the one named last changes fastest.
Arguments:
- features: bfloat16 [100, 8192], P('feat', 'node'), may hold values from -6 to 6
- edges_one: int32 [1024, 8192], P(None, 'node'), may hold values from 0 to 1, as said below
- w1_self: bfloat16 [100, 256], P('feat'), may hold values from -0.625 to 0.625
- w1_nbr: bfloat16 [100, 256], P('feat'), may hold values from -1.25 to 1.25
- need_blocks: int32 [8, 4], P('node'), may hold values from 0 to 7, as said below
- live_slots: int32 [8, 4], P('node'), may hold values from 0 to 1, as said below
- edges_two: int32 [4096, 8192], P(None, 'node'), may hold values from 0 to 1, as said below
- w2_self: bfloat16 [256, 47], P('feat'), may hold values from -0.375 to 0.375
- w2_nbr: bfloat16 [256, 47], P('feat'), may hold values from -0.5 to 0.5
- labels: int32 [8192], P('node'), may hold values from 0 to 46
Outputs:
- node_loss: float32 [8192], P('node')
- mean_loss: float32 [], replicated
Inputs may be any that keep to these rules, and one draw needn't show every extreme that they name: `need_blocks`: row b holds 4 different blocks; its first entry is b, its second is b plus half the number of blocks, its third is b minus 1, and its entry k is b plus an offset that depends on k alone, modulo the number of blocks. `live_slots`: the first three entries of each row are 1. `edges_one`: each column has exactly 25 ones. `edges_two`: each column t has exactly 10 ones, all in rows of slots that live_slots marks as used for t's block.
All inputs are finite; a program needn't handle non-finite values.
Results may differ from a plain program's by a relative error of at most 0.00065.
Values may be sent and summed in bfloat16 or wider, within the bound.
A program may use at most 128 MiB of HBM per device.

v0:
```python
import jax
import jax.numpy as jnp
from jax import lax
from jax.sharding import PartitionSpec as P

FAN1 = 25
FAN2 = 10


def from_behind(value, axis, steps):
    count = lax.axis_size(axis)
    pairs = [(source, (source + steps) % count) for source in range(count)]
    return lax.ppermute(value, axis, pairs)


def contract(weight, values):
    return lax.dot_general(
        weight, values, (((0,), (0,)), ((), ())), preferred_element_type=jnp.float32
    )


def contract_exact(weight, values):
    return lax.dot_general(
        weight,
        values,
        (((0,), (0,)), ((), ())),
        precision=lax.Precision.HIGHEST,
        preferred_element_type=jnp.float32,
    )


def fetch_offset(hidden, offset):
    nodes = lax.axis_size("node")
    levels = nodes.bit_length() - 1
    carried = hidden
    for level_bit in range(levels):
        moved = from_behind(carried, "node", nodes - (1 << level_bit))
        carried = jnp.where(offset // (1 << level_bit) % 2 == 1, moved, carried)
    return carried


def local(
    features,
    edges_one,
    w1_self,
    w1_nbr,
    need_blocks,
    live_slots,
    edges_two,
    w2_self,
    w2_nbr,
    labels,
):
    block_len = features.shape[1]
    classes = w2_self.shape[1]
    adjacency = edges_one.astype(jnp.bfloat16)
    neighbour = (jnp.dot(features, adjacency, preferred_element_type=jnp.float32) / FAN1).astype(
        jnp.bfloat16
    )
    before = lax.psum_scatter(
        contract(w1_self, features) + contract(w1_nbr, neighbour),
        "feat",
        scatter_dimension=0,
        tiled=True,
    )
    hidden = jax.nn.relu(before).astype(jnp.bfloat16)
    need_row = need_blocks[0]
    live_row = live_slots[0]
    self_term = contract(w2_self, hidden)
    nodes = lax.axis_size("node")
    mine_index = lax.axis_index("node")
    first_rows = edges_two[0:block_len].astype(jnp.bfloat16)
    gathered = jnp.dot(hidden, first_rows, preferred_element_type=jnp.float32)
    for slot in range(1, need_row.shape[0]):
        offset = (need_row[slot] - mine_index + nodes) % nodes
        sources = fetch_offset(hidden, offset)
        rows = edges_two[slot * block_len : (slot + 1) * block_len].astype(jnp.bfloat16)
        term = jnp.dot(sources, rows, preferred_element_type=jnp.float32)
        gathered = gathered + jnp.where(live_row[slot] == 1, term, 0.0)
    neighbour_term = contract_exact(w2_nbr.astype(jnp.float32), gathered)
    logits = lax.psum(self_term + neighbour_term / FAN2, "feat")
    class_ids = jnp.arange(classes, dtype=jnp.int32)[:, None]
    picked = jnp.sum(jnp.where(class_ids == labels[None, :], logits, 0.0), 0)
    node_loss = jnp.log(jnp.sum(jnp.exp(logits), 0)) - picked
    summed = lax.psum(jnp.sum(node_loss), "node")
    mean_loss = summed / (block_len * lax.axis_size("node"))
    return (node_loss, mean_loss)


def solution(mesh):
    return jax.shard_map(
        local,
        mesh=mesh,
        in_specs=(
            P("feat", "node"),
            P(None, "node"),
            P("feat", None),
            P("feat", None),
            P("node", None),
            P("node", None),
            P(None, "node"),
            P("feat", None),
            P("feat", None),
            P("node"),
        ),
        out_specs=(P("node"), P()),
        check_vma=False,
    )
```

profile of v0, /device:TPU:0, one launch (start us, length us, event | category | flops | bytes accessed | tf_op | source)
XLA Modules:
  0.0 156.6 jit_solution(11803071579191022002)
XLA Ops:
  7.2 0.8 copy-done
  8.0 1.0 fusion.49
  9.0 3.8 %fusion.10 = f32[256,1024]{1,0:T(8,128)} fusion(f32[256,1024]{1,0:T(8,128)S(1)} %fusion.49, bf16[25,256]{1,0:T(8,128)(2,1)} %param.13, bf16[25,1024]{1,0:T(8,128)(2,1)S(1)} %copy-done, s32[1024,1024]{1,0:T(8,128)} %param.11), kind=kOutput, calls=%fused_computation.11 | convolution fusion | flops 66897920 | bytes 6355456 | tf_op jit(solution)/shard_map/dot_general | solution.py:17
  13.0 27.6 %reduce-scatter.2.cloned.1.call-done = f32[64,1024]{1,0:T(8,128)} async-done(((f32[256,1024]{1,0:T(8,128)}), f32[64,1024]{1,0:T(8,128)}) %reduce-scatter.2.cloned.1.call-update) | async-done | bytes 262160 | tf_op jit(solution)/shard_map/reduce_scatter | solution.py:60
  40.6 1.0 maximum_convert_fusion
  41.5 4.3 %collective-permute-start = (bf16[64,1024]{1,0:T(8,128)(2,1)S(1)}, bf16[64,1024]{1,0:T(8,128)(2,1)S(1)}, u32[]{:S(2)}, u32[]{:S(2)}) collective-permute-start(bf16[64,1024]{1,0:T(8,128)(2,1)S(1)} %maximum_convert_fusion), channel_id=1, source_target_pairs={{0,28},{4,0},{8,4},{12,8},{16,12},{20,16},{24,20},{28,24},{1,29},{... | collective-permute-start | bytes 393224 | tf_op jit(solution)/shard_map/ppermute | solution.py:13
  45.8 0.6 fusion.48
  48.6 9.7 %convert.6 = bf16[4096,1024]{1,0:T(8,128)(2,1)} convert(s32[4096,1024]{1,0:T(8,128)} %param.16) | non-fusion elementwise | flops 4194304 | bytes 25165824 | tf_op jit(solution)/shard_map/convert.3
  58.3 0.6 fusion.47
  61.4 2.1 %fusion.6 = f32[64,1024]{1,0:T(8,128)S(1)} fusion(bf16[64,1024]{1,0:T(8,128)(2,1)S(1)} %maximum_convert_fusion, bf16[4096,1024]{1,0:T(8,128)(2,1)} %convert.6), kind=kOutput, calls=%fused_computation.6 | convolution fusion | flops 134217728 | bytes 2490368 | tf_op jit(solution)/shard_map/dot_general | solution.py:73
  64.5 1.8 %collective-permute-done.1 = bf16[64,1024]{1,0:T(8,128)(2,1)S(1)} collective-permute-done((bf16[64,1024]{1,0:T(8,128)(2,1)S(1)}, bf16[64,1024]{1,0:T(8,128)(2,1)S(1)}, u32[]{:S(2)}, u32[]{:S(2)}) %collective-permute-start.1) | collective-permute-done | bytes 131104 | tf_op jit(solution)/shard_map/ppermute | solution.py:13
  66.4 0.6 collective-permute-start.2
  67.1 2.8 %collective-permute-done.3 = bf16[64,1024]{1,0:T(8,128)(2,1)S(1)} collective-permute-done((bf16[64,1024]{1,0:T(8,128)(2,1)S(1)}, bf16[64,1024]{1,0:T(8,128)(2,1)S(1)}, u32[]{:S(2)}, u32[]{:S(2)}) %collective-permute-start.3) | collective-permute-done | bytes 131104 | tf_op jit(solution)/shard_map/ppermute | solution.py:13
  69.9 2.2 %collective-permute-start.4 = (bf16[64,1024]{1,0:T(8,128)(2,1)S(1)}, bf16[64,1024]{1,0:T(8,128)(2,1)S(1)}, u32[]{:S(2)}, u32[]{:S(2)}) collective-permute-start(bf16[64,1024]{1,0:T(8,128)(2,1)S(1)} %broadcast_select_fusion.3), channel_id=1, source_target_pairs={{0,16},{4,20},{8,24},{12,28},{16,0},{20,4},{24,8},{28,12},{1,17},{... | collective-permute-start | bytes 393224 | tf_op jit(solution)/shard_map/ppermute | solution.py:13
  72.1 6.8 %collective-permute-start.6 = (bf16[64,1024]{1,0:T(8,128)(2,1)S(1)}, bf16[64,1024]{1,0:T(8,128)(2,1)S(1)}, u32[]{:S(2)}, u32[]{:S(2)}) collective-permute-start(bf16[64,1024]{1,0:T(8,128)(2,1)S(1)} %broadcast_select_fusion.1), channel_id=1, source_target_pairs={{0,16},{4,20},{8,24},{12,28},{16,0},{20,4},{24,8},{28,12},{1,17},{... | collective-permute-start | bytes 393224 | tf_op jit(solution)/shard_map/ppermute | solution.py:13
  78.8 8.3 %collective-permute-done.4 = bf16[64,1024]{1,0:T(8,128)(2,1)S(1)} collective-permute-done((bf16[64,1024]{1,0:T(8,128)(2,1)S(1)}, bf16[64,1024]{1,0:T(8,128)(2,1)S(1)}, u32[]{:S(2)}, u32[]{:S(2)}) %collective-permute-start.4) | collective-permute-done | bytes 131104 | tf_op jit(solution)/shard_map/ppermute | solution.py:13
  87.2 2.1 %fusion.20 = f32[64,1024]{1,0:T(8,128)S(1)} fusion(bf16[4096,1024]{1,0:T(8,128)(2,1)} %convert.6, bf16[64,1024]{1,0:T(8,128)(2,1)S(1)} %collective-permute-done.4, bf16[64,1024]{1,0:T(8,128)(2,1)S(1)} %broadcast_select_fusion.3, pred[]{:T(512)S(6)} %eq.78, pred[]{:T(512)} %bitcast.3), kind=kOutput, calls=%fused_computation.15 | convolution fusion | flops 134348800 | bytes 2621953 | tf_op jit(solution)/shard_map/dot_general | solution.py:78
  89.3 2.1 %fusion.23 = f32[64,1024]{1,0:T(8,128)S(1)} fusion(bf16[4096,1024]{1,0:T(8,128)(2,1)} %convert.6, bf16[64,1024]{1,0:T(8,128)(2,1)S(1)} %collective-permute-done.6, bf16[64,1024]{1,0:T(8,128)(2,1)S(1)} %broadcast_select_fusion.1, pred[]{:T(512)S(6)} %eq.83, pred[]{:T(512)} %bitcast.5), kind=kOutput, calls=%fused_computation.16 | convolution fusion | flops 134348800 | bytes 2621953 | tf_op jit(solution)/shard_map/dot_general | solution.py:78
  91.4 2.1 %fusion.26 = f32[64,1024]{1,0:T(8,128)S(1)} fusion(f32[64,1024]{1,0:T(8,128)S(1)} %fusion.23, f32[64,1024]{1,0:T(8,128)S(1)} %fusion.20, f32[64,1024]{1,0:T(8,128)S(1)} %fusion.6, bf16[4096,1024]{1,0:T(8,128)(2,1)} %convert.6, bf16[64,1024]{1,0:T(8,128)(2,1)S(1)} %collective-permute-done.2, bf16[64,1024]{1,0:T(8,128)(2,1)S(1)} %broadcast_select_fusion.5, ...), kind=kOutput, calls=%fused_computation.17 | convolution fusion | flops 134545408 | bytes 3408385 | tf_op jit(solution)/shard_map/dot_general | solution.py:78
  93.8 0.8 fusion.29
  94.6 29.2 %all-reduce.2.cloned.1.call-done = f32[47,1024]{1,0:T(8,128)} async-done(((f32[47,1024]{1,0:T(8,128)}), f32[47,1024]{1,0:T(8,128)}) %all-reduce.2.cloned.1.call-update) | async-done | bytes 192528 | tf_op jit(solution)/shard_map/psum | solution.py:81
  123.9 1.0 exponential_reduce_fusion
  124.8 1.2 fusion.46
  126.0 22.0 %psum.15 = f32[]{:T(128)} all-reduce(f32[]{:T(128)} %get-tuple-element.4), channel_id=1, replica_groups=mesh['node'=8,'feat'=4] {'node'}, use_global_device_ids=true, to_apply=%region_5.6 | all-reduce | flops 1 | bytes 8 | tf_op jit(solution)/shard_map/psum | solution.py:85
  (29 shorter events, 2.2 us)
Async XLA Ops:
  7.2 0.8 copy-start
  7.2 38.7 %copy-start.4 = (s32[1,4]{1,0:T(1,128)S(1)}, s32[1,4]{1,0:T(1,128)}, u32[]{:S(2)}) copy-start(s32[1,4]{1,0:T(1,128)} %param.14) | copy-start | bytes 52
  7.2 33.4 %reduce-scatter.2.cloned.1.call-start = ((), (), s32[]{:S(2)}) async-start(), calls=%async_computation.1 | async-start | bytes 1310720 | tf_op jit(solution)/shard_map/reduce_scatter | solution.py:60
  12.9 110.9 %all-reduce.2.cloned.1.call-start = ((), (), s32[]{:S(2)}) async-start(), calls=%async_computation.2 | async-start | bytes 393216 | tf_op jit(solution)/shard_map/psum | solution.py:81
  41.5 19.2 %collective-permute-start = (bf16[64,1024]{1,0:T(8,128)(2,1)S(1)}, bf16[64,1024]{1,0:T(8,128)(2,1)S(1)}, u32[]{:S(2)}, u32[]{:S(2)}) collective-permute-start(bf16[64,1024]{1,0:T(8,128)(2,1)S(1)} %maximum_convert_fusion), channel_id=1, source_target_pairs={{0,28},{4,0},{8,4},{12,8},{16,12},{20,16},{24,20},{28,24},{1,29},{... | collective-permute-start | bytes 393224 | tf_op jit(solution)/shard_map/ppermute | solution.py:13
  48.5 9.7 %copy-start.5 = (s32[1,4]{1,0:T(1,128)S(1)}, s32[1,4]{1,0:T(1,128)}, u32[]{:S(2)}) copy-start(s32[1,4]{1,0:T(1,128)} %param.15) | copy-start | bytes 52
  48.6 12.2 %copy-start.1 = (f32[64,1024]{1,0:T(8,128)S(1)}, f32[64,1024]{1,0:T(8,128)}, u32[]{:S(2)}) copy-start(f32[64,1024]{1,0:T(8,128)} %reduce-scatter.2.cloned.1.call-done) | copy-start | bytes 786436
  60.8 5.6 %collective-permute-start.1 = (bf16[64,1024]{1,0:T(8,128)(2,1)S(1)}, bf16[64,1024]{1,0:T(8,128)(2,1)S(1)}, u32[]{:S(2)}, u32[]{:S(2)}) collective-permute-start(bf16[64,1024]{1,0:T(8,128)(2,1)S(1)} %get-tuple-element.6), channel_id=1, source_target_pairs={{0,24},{4,28},{8,0},{12,4},{16,8},{20,12},{24,16},{28,20},{1,25},{... | collective-permute-start | bytes 393224 | tf_op jit(solution)/shard_map/ppermute | solution.py:13
  63.4 6.4 %collective-permute-start.3 = (bf16[64,1024]{1,0:T(8,128)(2,1)S(1)}, bf16[64,1024]{1,0:T(8,128)(2,1)S(1)}, u32[]{:S(2)}, u32[]{:S(2)}) collective-permute-start(bf16[64,1024]{1,0:T(8,128)(2,1)S(1)} %get-tuple-element.8), channel_id=1, source_target_pairs={{0,24},{4,28},{8,0},{12,4},{16,8},{20,12},{24,16},{28,20},{1,25},{... | collective-permute-start | bytes 393224 | tf_op jit(solution)/shard_map/ppermute | solution.py:13
  64.0 8.0 %collective-permute-start.5 = (bf16[64,1024]{1,0:T(8,128)(2,1)S(1)}, bf16[64,1024]{1,0:T(8,128)(2,1)S(1)}, u32[]{:S(2)}, u32[]{:S(2)}) collective-permute-start(bf16[64,1024]{1,0:T(8,128)(2,1)S(1)} %get-tuple-element.7), channel_id=1, source_target_pairs={{0,24},{4,28},{8,0},{12,4},{16,8},{20,12},{24,16},{28,20},{1,25},{... | collective-permute-start | bytes 393224 | tf_op jit(solution)/shard_map/ppermute | solution.py:13
  66.4 25.0 %collective-permute-start.2 = (bf16[64,1024]{1,0:T(8,128)(2,1)S(1)}, bf16[64,1024]{1,0:T(8,128)(2,1)S(1)}, u32[]{:S(2)}, u32[]{:S(2)}) collective-permute-start(bf16[64,1024]{1,0:T(8,128)(2,1)S(1)} %broadcast_select_fusion.5), channel_id=1, source_target_pairs={{0,16},{4,20},{8,24},{12,28},{16,0},{20,4},{24,8},{28,12},{1,17},{... | collective-permute-start | bytes 393224 | tf_op jit(solution)/shard_map/ppermute | solution.py:13
  69.9 17.3 %collective-permute-start.4 = (bf16[64,1024]{1,0:T(8,128)(2,1)S(1)}, bf16[64,1024]{1,0:T(8,128)(2,1)S(1)}, u32[]{:S(2)}, u32[]{:S(2)}) collective-permute-start(bf16[64,1024]{1,0:T(8,128)(2,1)S(1)} %broadcast_select_fusion.3), channel_id=1, source_target_pairs={{0,16},{4,20},{8,24},{12,28},{16,0},{20,4},{24,8},{28,12},{1,17},{... | collective-permute-start | bytes 393224 | tf_op jit(solution)/shard_map/ppermute | solution.py:13
  72.1 17.2 %collective-permute-start.6 = (bf16[64,1024]{1,0:T(8,128)(2,1)S(1)}, bf16[64,1024]{1,0:T(8,128)(2,1)S(1)}, u32[]{:S(2)}, u32[]{:S(2)}) collective-permute-start(bf16[64,1024]{1,0:T(8,128)(2,1)S(1)} %broadcast_select_fusion.1), channel_id=1, source_target_pairs={{0,16},{4,20},{8,24},{12,28},{16,0},{20,4},{24,8},{28,12},{1,17},{... | collective-permute-start | bytes 393224 | tf_op jit(solution)/shard_map/ppermute | solution.py:13
  87.2 6.3 %copy-start.2 = (bf16[64,47]{0,1:T(8,128)(2,1)S(1)}, bf16[64,47]{0,1:T(8,128)(2,1)}, u32[]{:S(2)}) copy-start(bf16[64,47]{0,1:T(8,128)(2,1)} %param.18) | copy-start | bytes 18052
  87.2 6.6 %copy-start.3 = (bf16[64,47]{0,1:T(8,128)(2,1)S(1)}, bf16[64,47]{0,1:T(8,128)(2,1)}, u32[]{:S(2)}) copy-start(bf16[64,47]{0,1:T(8,128)(2,1)} %param.17) | copy-start | bytes 18052
  89.3 34.6 %copy-start.6 = (s32[1024]{0:T(1024)S(1)}, s32[1024]{0:T(1024)}, u32[]{:S(2)}) copy-start(s32[1024]{0:T(1024)} %param.19) | copy-start | bytes 12292
Sparse Core Ops, SparseCore 0:
  13.0 27.4 reduce-scatter.1
  94.7 29.0 all-reduce.1
where the time goes:
time: 157 us
  waiting for transfers between devices  69.8 us (44%)
  blocking collectives  22 us (14%)
  between operations  20 us (13%)
  starting transfers between devices  15.7 us (10%)
  matrix products  14.3 us (9%)
  other arithmetic  12.9 us (8%)
  local copies, waits for them, and re-layouts  1.99 us (1%)
    psum x1, waiting for transfers between devices, local(): logits = lax.psum(self_term + neighbour_term / FAN2, 'feat')  29.2 us
    reduce_scatter x1, waiting for transfers between devices, local(): lax.psum_scatter(contract(w1_self, features) + contract(w1_nbr, neighbour...  27.6 us
    psum x1, blocking collectives, local(): summed = lax.psum(jnp.sum(node_loss), 'node')  22 us
    ppermute x7, starting transfers between devices, from_behind(): return lax.ppermute(value, axis, pairs)  15.6 us
    ppermute x7, waiting for transfers between devices, from_behind(): return lax.ppermute(value, axis, pairs)  13 us
    another operation x1, other arithmetic  9.68 us
    dot_general x3, matrix products, local(): term = jnp.dot(sources, rows, preferred_element_type=jnp.float32)  6.26 us
    dot_general x3, matrix products, contract(): lax.dot_general(weight, values, (((0,), (0,)), ((), ())), preferred_eleme...  5.7 us
  transfers between devices with their start and end apart: 9, of which 5 were waited for; matrix products, arithmetic and copies ran while one was open for 11% of the time, Pallas kernels for 0%

commit v1 on v0

v1 whole, which is shorter than its diff:
```python
import functools

import jax
import jax.numpy as jnp
from jax import lax
from jax.experimental import pallas as pl
from jax.experimental.pallas import tpu as pltpu
from jax.sharding import PartitionSpec as P

FAN1 = 25
FAN2 = 10
MESH = pl.DeviceIdType.MESH


def kernel(
    nodes,
    feats,
    features,
    edges_one,
    w1_self,
    w1_nbr,
    need,
    live,
    edges_two,
    w2_self,
    w2_nbr,
    labels,
    loss_out,
    mean_out,
    feat_full,
    edge1,
    edge2,
    lab,
    w1s_all,
    w1n_all,
    w2s_all,
    w2n_all,
    feat_all,
    agg_own,
    agg_all,
    p_all,
    part,
    part_all,
    loss_all,
    load_sem,
    edge1_sem,
    edge2_sem,
    a_send,
    a_recv,
    p_send,
    p_recv,
    c_send,
    c_recv,
    d_send,
    d_recv,
):
    node = lax.axis_index("node")
    feat = lax.axis_index("feat")
    block = feat_full.shape[1]
    quarter = block // feats
    slots = edges_two.shape[0] // block
    e1_chunks = edge1.shape[0]
    e1_rows = edge1.shape[1]

    def cols(index):
        return pl.ds(pl.multiple_of(index * quarter, quarter), quarter)

    def remote(src, dst, send, recv, node_id, feat_id):
        return pltpu.make_async_remote_copy(
            src_ref=src,
            dst_ref=dst,
            send_sem=send,
            recv_sem=recv,
            device_id={"node": node_id, "feat": feat_id},
            device_id_type=MESH,
        )

    loads = [
        pltpu.make_async_copy(features, feat_full, load_sem.at[0]),
        pltpu.make_async_copy(w1_self, w1s_all.at[feat], load_sem.at[1]),
        pltpu.make_async_copy(w1_nbr, w1n_all.at[feat], load_sem.at[2]),
        pltpu.make_async_copy(w2_self, w2s_all.at[feat], load_sem.at[3]),
        pltpu.make_async_copy(w2_nbr, w2n_all.at[feat], load_sem.at[4]),
        pltpu.make_async_copy(labels, lab, load_sem.at[5]),
    ]
    for copy in loads:
        copy.start()
    e1_loads = [
        pltpu.make_async_copy(
            edges_one.at[pl.ds(c * e1_rows, e1_rows), :], edge1.at[c], edge1_sem.at[c]
        )
        for c in range(e1_chunks)
    ]
    for copy in e1_loads:
        copy.start()
    e2_loads = [
        pltpu.make_async_copy(
            edges_two.at[pl.ds(pl.multiple_of(k * block + feat * quarter, quarter), quarter), :],
            edge2.at[k],
            edge2_sem.at[k],
        )
        for k in range(slots)
    ]
    for copy in e2_loads:
        copy.start()

    barrier = pltpu.get_barrier_semaphore()
    others = [
        (dn, df) for dn in range(nodes) for df in range(feats) if dn or df
    ]
    for dn, df in others:
        pl.semaphore_signal(
            barrier,
            inc=1,
            device_id={
                "node": lax.rem(node + dn, nodes),
                "feat": lax.rem(feat + df, feats),
            },
            device_id_type=MESH,
        )

    loads[0].wait()
    total = None
    for c in range(e1_chunks):
        e1_loads[c].wait()
        term = jnp.dot(
            feat_full[:, c * e1_rows : (c + 1) * e1_rows],
            edge1[c].astype(jnp.bfloat16),
            preferred_element_type=jnp.float32,
        )
        total = term if total is None else total + term
    agg_own[...] = (total / FAN1).astype(jnp.bfloat16)
    for copy in loads[1:]:
        copy.wait()

    pl.semaphore_wait(barrier, len(others))

    sent = []
    arrivals = {}
    groups = [
        (0, lambda to: feat_full.at[:, cols(to)], lambda who: feat_all.at[who]),
        (1, lambda to: agg_own.at[:, cols(to)], lambda who: agg_all.at[who]),
        (2, lambda to: w1s_all.at[feat], lambda who: w1s_all.at[who]),
        (3, lambda to: w1n_all.at[feat], lambda who: w1n_all.at[who]),
        (4, lambda to: w2n_all.at[feat], lambda who: w2n_all.at[who]),
        (5, lambda to: w2s_all.at[feat], lambda who: w2s_all.at[who]),
    ]
    for item, source, target in groups:
        for df in range(1, feats):
            to = lax.rem(feat + df, feats)
            come = lax.rem(feat + feats - df, feats)
            copy = remote(
                source(to), target(feat), a_send.at[item, df], a_recv.at[item, df], node, to
            )
            copy.start()
            sent.append(copy)
            arrivals[item, df] = remote(
                source(to), target(come), a_send.at[item, df], a_recv.at[item, df], node, to
            )

    def contract(weight, values):
        return lax.dot_general(
            weight, values, (((0,), (0,)), ((), ())), preferred_element_type=jnp.float32
        )

    before = contract(w1s_all[feat], feat_full[:, cols(feat)])
    before = before + contract(w1n_all[feat], agg_own[:, cols(feat)])
    for df in range(1, feats):
        come = lax.rem(feat + feats - df, feats)
        arrivals[0, df].wait_recv()
        arrivals[2, df].wait_recv()
        before = before + contract(w1s_all[come], feat_all[come])
        arrivals[1, df].wait_recv()
        arrivals[3, df].wait_recv()
        before = before + contract(w1n_all[come], agg_all[come])
    hidden = jnp.maximum(before, 0.0).astype(jnp.bfloat16)

    share = hidden.shape[0] // feats
    for df in range(1, feats):
        arrivals[4, df].wait_recv()
    projected = None
    for who in range(feats):
        term = jnp.dot(
            w2n_all[who],
            hidden[who * share : (who + 1) * share],
            preferred_element_type=jnp.float32,
        )
        projected = term if projected is None else projected + term
    p_all[node] = projected.astype(p_all.dtype)

    p_arrive = {}
    for dn in range(1, nodes):
        to = lax.rem(node + dn, nodes)
        come = lax.rem(node + nodes - dn, nodes)
        copy = remote(p_all.at[node], p_all.at[node], p_send.at[dn], p_recv.at[dn], to, feat)
        copy.start()
        sent.append(copy)
        p_arrive[dn] = remote(
            p_all.at[node], p_all.at[come], p_send.at[dn], p_recv.at[dn], to, feat
        )

    for df in range(1, feats):
        arrivals[5, df].wait_recv()
    self_term = None
    for who in range(feats):
        term = jnp.dot(
            w2s_all[who],
            hidden[who * share : (who + 1) * share],
            preferred_element_type=jnp.float32,
        )
        self_term = term if self_term is None else self_term + term

    def gather(k, values):
        return jnp.dot(
            values, edge2[k].astype(jnp.bfloat16), preferred_element_type=jnp.float32
        )

    e2_loads[0].wait()
    gathered = gather(0, p_all[node])
    half = nodes // 2
    e2_loads[2].wait()
    p_arrive[1].wait_recv()
    gathered = gathered + gather(2, p_all[lax.rem(node + nodes - 1, nodes)])
    e2_loads[1].wait()
    if half != 1:
        p_arrive[half].wait_recv()
    gathered = gathered + gather(1, p_all[lax.rem(node + half, nodes)])
    for dn in range(1, nodes):
        if dn not in (1, half):
            p_arrive[dn].wait_recv()
    for k in range(3, slots):
        e2_loads[k].wait()
        values = p_all[need[0, k]]
        values = jnp.where(live[0, k] == 1, values, jnp.zeros_like(values))
        gathered = gathered + gather(k, values)
    part[...] = gathered

    c_arrive = {}
    for df in range(1, feats):
        to = lax.rem(feat + df, feats)
        come = lax.rem(feat + feats - df, feats)
        copy = remote(
            part.at[:, cols(to)], part_all.at[feat], c_send.at[df], c_recv.at[df], node, to
        )
        copy.start()
        sent.append(copy)
        c_arrive[df] = remote(
            part.at[:, cols(to)], part_all.at[come], c_send.at[df], c_recv.at[df], node, to
        )
    summed = part[:, cols(feat)]
    for df in range(1, feats):
        come = lax.rem(feat + feats - df, feats)
        c_arrive[df].wait_recv()
        summed = summed + part_all[come]
    logits = self_term + summed / FAN2
    class_ids = lax.broadcasted_iota(jnp.int32, logits.shape, 0)
    picked = jnp.sum(
        jnp.where(class_ids == lab[:, cols(feat)], logits, 0.0), axis=0, keepdims=True
    )
    loss = jnp.log(jnp.sum(jnp.exp(logits), axis=0, keepdims=True)) - picked
    mine = node * feats + feat
    loss_all[mine] = loss

    d_arrive = []
    for index, (dn, df) in enumerate(others):
        to_node = lax.rem(node + dn, nodes)
        to_feat = lax.rem(feat + df, feats)
        come = lax.rem(node + nodes - dn, nodes) * feats + lax.rem(feat + feats - df, feats)
        copy = remote(
            loss_all.at[mine], loss_all.at[mine], d_send.at[index], d_recv.at[index], to_node, to_feat
        )
        copy.start()
        sent.append(copy)
        d_arrive.append(
            remote(
                loss_all.at[mine], loss_all.at[come], d_send.at[index], d_recv.at[index], to_node, to_feat
            )
        )
    for copy in d_arrive:
        copy.wait_recv()
    for who in range(feats):
        loss_out[:, who * quarter : (who + 1) * quarter] = loss_all[node * feats + who]
    total_loss = jnp.sum(loss_all[...])
    mean_out[0, 0] = total_loss / (block * nodes)
    for copy in sent:
        copy.wait_send()


def local(nodes, feats, features, edges_one, w1_self, w1_nbr, need, live, edges_two, w2_self, w2_nbr, labels):
    rows, block = features.shape
    hidden = w1_self.shape[1]
    share, classes = w2_self.shape
    quarter = block // feats
    slots = need.shape[1]
    chunks = 4
    ndev = nodes * feats
    bf16, f32, i32 = jnp.bfloat16, jnp.float32, jnp.int32
    anywhere = pl.BlockSpec(memory_space=pl.ANY)
    scalar = pl.BlockSpec(memory_space=pltpu.SMEM)
    sems = pltpu.SemaphoreType.DMA
    loss, mean = pl.pallas_call(
        functools.partial(kernel, nodes, feats),
        out_shape=(
            jax.ShapeDtypeStruct((1, block), f32),
            jax.ShapeDtypeStruct((1, 1), f32),
        ),
        in_specs=[
            anywhere,
            anywhere,
            anywhere,
            anywhere,
            scalar,
            scalar,
            anywhere,
            anywhere,
            anywhere,
            anywhere,
        ],
        out_specs=(pl.BlockSpec(memory_space=pltpu.VMEM), scalar),
        scratch_shapes=[
            pltpu.VMEM((rows, block), bf16),
            pltpu.VMEM((chunks, block // chunks, block), i32),
            pltpu.VMEM((slots, quarter, block), i32),
            pltpu.VMEM((1, block), i32),
            pltpu.VMEM((feats, rows, hidden), bf16),
            pltpu.VMEM((feats, rows, hidden), bf16),
            pltpu.VMEM((feats, classes, share), bf16),
            pltpu.VMEM((feats, classes, share), bf16),
            pltpu.VMEM((feats, rows, quarter), bf16),
            pltpu.VMEM((rows, block), bf16),
            pltpu.VMEM((feats, rows, quarter), bf16),
            pltpu.VMEM((nodes, classes, quarter), bf16),
            pltpu.VMEM((classes, block), f32),
            pltpu.VMEM((feats, classes, quarter), f32),
            pltpu.VMEM((ndev, 1, quarter), f32),
            sems((6,)),
            sems((chunks,)),
            sems((slots,)),
            sems((6, feats)),
            sems((6, feats)),
            sems((nodes,)),
            sems((nodes,)),
            sems((feats,)),
            sems((feats,)),
            sems((ndev,)),
            sems((ndev,)),
        ],
        compiler_params=pltpu.CompilerParams(
            collective_id=0,
            has_side_effects=True,
            vmem_limit_bytes=40 * 1024 * 1024,
        ),
    )(
        features,
        edges_one,
        w1_self,
        w1_nbr,
        need,
        live,
        edges_two,
        w2_self.T,
        w2_nbr.T,
        labels.reshape(1, block),
    )
    return loss.reshape(block), mean.reshape(())


def solution(mesh):
    return jax.shard_map(
        functools.partial(local, mesh.shape["node"], mesh.shape["feat"]),
        mesh=mesh,
        in_specs=(
            P("feat", "node"),
            P(None, "node"),
            P("feat", None),
            P("feat", None),
            P("node", None),
            P("node", None),
            P(None, "node"),
            P("feat", None),
            P("feat", None),
            P("node"),
        ),
        out_specs=(P("node"), P()),
        check_vma=False,
    )
```

time: 157 us -> 41.3 us (0.26)
  waiting for transfers between devices: 69.8 us -> 0 us
  Pallas kernels: 0 us -> 29.9 us
  blocking collectives: 22 us -> 0 us
  between operations: 20 us -> 2.41 us
  starting transfers between devices: 15.7 us -> 0 us
  matrix products: 14.3 us -> 0 us
  other arithmetic: 12.9 us -> 0 us
  local copies, waits for them, and re-layouts: 1.99 us -> 8.46 us
    pallas_call x0 -> x1, Pallas kernels: none -> 29.9 us  [local(): pl.pallas_call(functools.partial(kernel, nodes, feats), out_shape=(jax.Sh...]
    psum x1 -> x0, waiting for transfers between devices: 29.2 us -> none  [local(): logits = lax.psum(self_term + neighbour_term / FAN2, 'feat')]
    reduce_scatter x1 -> x0, waiting for transfers between devices: 27.6 us -> none  [local(): lax.psum_scatter(contract(w1_self, features) + contract(w1_nbr, neighbour...]
    psum x1 -> x0, blocking collectives: 22 us -> none  [local(): summed = lax.psum(jnp.sum(node_loss), 'node')]
    ppermute x7 -> x0, starting transfers between devices: 15.6 us -> none  [from_behind(): return lax.ppermute(value, axis, pairs)]
    dot_general x8 -> x0, matrix products: 14.3 us -> none  [the longest x3 6.26 us: local(): term = jnp.dot(sources, rows, preferred_element_type=jnp.float32)]
    ppermute x7 -> x0, waiting for transfers between devices: 13 us -> none  [from_behind(): return lax.ppermute(value, axis, pairs)]
    another operation x1 -> x0, other arithmetic: 9.68 us -> none
  transfers between devices with their start and end apart: 9 -> 0, of which waited for: 5 -> 0; matrix products, arithmetic and copies ran while one was open for 11% -> 0% of each run, Pallas kernels for 0% -> 0%
where the time goes in v1:
time: 41.3 us; the launch traced here: 40.7 us
  Pallas kernels  29.9 us (72%)
  local copies, waits for them, and re-layouts  8.46 us (20%)
  between operations  2.41 us (6%)
    pallas_call x1, Pallas kernels, local(): pl.pallas_call(functools.partial(kernel, nodes, feats), out_shape=(jax.Sh...  29.9 us
    unnamed x19, local copies, waits for them, and re-layouts  8.46 us

profile of v1, /device:TPU:0, one launch (start us, length us, event | category | flops | bytes accessed | tf_op | source)
XLA Modules:
  0.0 40.7 jit_solution(11016054313829761952)
XLA Ops:
  0.6 0.0 copy-start
  0.6 2.2 %copy-done = s32[1024,1024]{1,0:T(8,128)S(1)} copy-done((s32[1024,1024]{1,0:T(8,128)S(1)}, s32[1024,1024]{1,0:T(8,128)}, u32[]{:S(2)}) %copy-start) | copy-done | bytes 4194328
  2.8 0.0 copy-start.1
  2.8 0.8 %copy-done.1 = bf16[25,1024]{1,0:T(8,128)(2,1)S(1)} copy-done((bf16[25,1024]{1,0:T(8,128)(2,1)S(1)}, bf16[25,1024]{1,0:T(8,128)(2,1)}, u32[]{:S(2)}) %copy-start.1) | copy-done | bytes 51224
  3.7 0.0 copy-start.2
  3.7 0.7 %copy-done.2 = bf16[25,256]{1,0:T(8,128)(2,1)S(1)} copy-done((bf16[25,256]{1,0:T(8,128)(2,1)S(1)}, bf16[25,256]{1,0:T(8,128)(2,1)}, u32[]{:S(2)}) %copy-start.2) | copy-done | bytes 12824
  4.4 0.0 copy-start.3
  4.4 0.7 %copy-done.3 = bf16[25,256]{1,0:T(8,128)(2,1)S(1)} copy-done((bf16[25,256]{1,0:T(8,128)(2,1)S(1)}, bf16[25,256]{1,0:T(8,128)(2,1)}, u32[]{:S(2)}) %copy-start.3) | copy-done | bytes 12824
  5.1 0.0 copy-start.4
  5.1 0.7 %copy-done.4 = bf16[64,47]{0,1:T(8,128)(2,1)S(1)} copy-done((bf16[64,47]{0,1:T(8,128)(2,1)S(1)}, bf16[64,47]{0,1:T(8,128)(2,1)}, u32[]{:S(2)}) %copy-start.4) | copy-done | bytes 6040
  5.8 0.0 copy-start.5
  5.8 0.7 %copy-done.5 = bf16[64,47]{0,1:T(8,128)(2,1)S(1)} copy-done((bf16[64,47]{0,1:T(8,128)(2,1)S(1)}, bf16[64,47]{0,1:T(8,128)(2,1)}, u32[]{:S(2)}) %copy-start.5) | copy-done | bytes 6040
  6.5 0.0 copy-start.6
  6.5 0.7 %copy-done.6 = s32[1024]{0:T(1024)S(1)} copy-done((s32[1024]{0:T(1024)S(1)}, s32[1024]{0:T(1024)}, u32[]{:S(2)}) %copy-start.6) | copy-done | bytes 4120
  7.2 0.0 copy-start.7
  7.2 0.7 %copy-done.7 = s32[1,4]{1,0:T(1,128)S(1)} copy-done((s32[1,4]{1,0:T(1,128)S(1)}, s32[1,4]{1,0:T(1,128)}, u32[]{:S(2)}) %copy-start.7) | copy-done | bytes 40
  7.9 0.0 copy-start.8
  7.9 0.7 %copy-done.8 = s32[1,4]{1,0:T(1,128)S(1)} copy-done((s32[1,4]{1,0:T(1,128)S(1)}, s32[1,4]{1,0:T(1,128)}, u32[]{:S(2)}) %copy-start.8) | copy-done | bytes 40
  8.5 29.9 %shard_map.113 = (f32[1,1024]{1,0:T(1,128)S(1)}, f32[1,1]{1,0:T(1,128)}) custom-call(bf16[25,1024]{1,0:T(8,128)(2,1)S(1)} %copy-done.1, s32[1024,1024]{1,0:T(8,128)S(1)} %copy-done, bf16[25,256]{1,0:T(8,128)(2,1)S(1)} %copy-done.2, bf16[25,256]{1,0:T(8,128)(2,1)S(1)} %copy-done.3, s32[1,4]{1,0:T(1,128)S(1)} %copy-done.7, s32[1,4]{1,0:T(1,128)S(1)} %copy-done.8, ...), custom_call_target="tpu_custom_call" | custom-call | tf_op jit(solution)/shard_map/pallas_call | solution.py:301
  38.4 0.6 %copy.14 = f32[1024]{0:T(1024)} copy(f32[1024]{0:T(1024)S(1)} %bitcast.8) | data formatting | bytes 8192
Async XLA Ops:
  0.6 2.2 %copy-start = (s32[1024,1024]{1,0:T(8,128)S(1)}, s32[1024,1024]{1,0:T(8,128)}, u32[]{:S(2)}) copy-start(s32[1024,1024]{1,0:T(8,128)} %edges_one.1) | copy-start | bytes 12582916
  2.8 0.8 %copy-start.1 = (bf16[25,1024]{1,0:T(8,128)(2,1)S(1)}, bf16[25,1024]{1,0:T(8,128)(2,1)}, u32[]{:S(2)}) copy-start(bf16[25,1024]{1,0:T(8,128)(2,1)} %features.1) | copy-start | bytes 153604
  3.7 0.7 %copy-start.2 = (bf16[25,256]{1,0:T(8,128)(2,1)S(1)}, bf16[25,256]{1,0:T(8,128)(2,1)}, u32[]{:S(2)}) copy-start(bf16[25,256]{1,0:T(8,128)(2,1)} %w1_self.1) | copy-start | bytes 38404
  4.4 0.7 %copy-start.3 = (bf16[25,256]{1,0:T(8,128)(2,1)S(1)}, bf16[25,256]{1,0:T(8,128)(2,1)}, u32[]{:S(2)}) copy-start(bf16[25,256]{1,0:T(8,128)(2,1)} %w1_nbr.1) | copy-start | bytes 38404
  5.1 0.7 %copy-start.4 = (bf16[64,47]{0,1:T(8,128)(2,1)S(1)}, bf16[64,47]{0,1:T(8,128)(2,1)}, u32[]{:S(2)}) copy-start(bf16[64,47]{0,1:T(8,128)(2,1)} %param.17) | copy-start | bytes 18052
  5.8 0.7 %copy-start.5 = (bf16[64,47]{0,1:T(8,128)(2,1)S(1)}, bf16[64,47]{0,1:T(8,128)(2,1)}, u32[]{:S(2)}) copy-start(bf16[64,47]{0,1:T(8,128)(2,1)} %param.18) | copy-start | bytes 18052
  6.5 0.7 %copy-start.6 = (s32[1024]{0:T(1024)S(1)}, s32[1024]{0:T(1024)}, u32[]{:S(2)}) copy-start(s32[1024]{0:T(1024)} %param.19) | copy-start | bytes 12292
  7.2 0.7 %copy-start.7 = (s32[1,4]{1,0:T(1,128)S(1)}, s32[1,4]{1,0:T(1,128)}, u32[]{:S(2)}) copy-start(s32[1,4]{1,0:T(1,128)} %need.1) | copy-start | bytes 52
  7.9 0.7 %copy-start.8 = (s32[1,4]{1,0:T(1,128)S(1)}, s32[1,4]{1,0:T(1,128)}, u32[]{:S(2)}) copy-start(s32[1,4]{1,0:T(1,128)} %live.1) | copy-start | bytes 52

commit v2 on v1

--- a/solution.py
+++ b/solution.py
@@ -53,6 +53,7 @@
     c_recv,
     d_send,
     d_recv,
+    ready,
 ):
     node = lax.axis_index("node")
     feat = lax.axis_index("feat")
@@ -101,39 +102,32 @@
         )
         for k in range(slots)
     ]
-    for copy in e2_loads:
-        copy.start()
-
     barrier = pltpu.get_barrier_semaphore()
-    others = [
-        (dn, df) for dn in range(nodes) for df in range(feats) if dn or df
-    ]
-    for dn, df in others:
+    odd = lax.rem(feat, 2)
+    partner = feat + 1 - 2 * odd
+
+    def greet(semaphore, to_node, to_feat):
         pl.semaphore_signal(
-            barrier,
+            semaphore,
             inc=1,
-            device_id={
-                "node": lax.rem(node + dn, nodes),
-                "feat": lax.rem(feat + df, feats),
-            },
+            device_id={"node": to_node, "feat": to_feat},
             device_id_type=MESH,
         )
 
-    loads[0].wait()
-    total = None
-    for c in range(e1_chunks):
-        e1_loads[c].wait()
-        term = jnp.dot(
-            feat_full[:, c * e1_rows : (c + 1) * e1_rows],
-            edge1[c].astype(jnp.bfloat16),
-            preferred_element_type=jnp.float32,
-        )
-        total = term if total is None else total + term
-    agg_own[...] = (total / FAN1).astype(jnp.bfloat16)
-    for copy in loads[1:]:
+    for df in range(1, feats):
+        to = lax.rem(feat + df, feats)
+        pl.when(lax.rem(to, 2) == 0)(functools.partial(greet, barrier, node, to))
+    for dn in range(1, nodes):
+        greet(barrier, lax.rem(node + dn, nodes), feat + 1 - odd)
+
+    def hear(count):
+        pl.semaphore_wait(barrier, count)
+        greet(ready, node, partner)
+
+    for copy in loads:
         copy.wait()
-
-    pl.semaphore_wait(barrier, len(others))
+    pl.when(odd == 0)(functools.partial(hear, feats - 1))
+    pl.when(odd == 1)(lambda: pl.semaphore_wait(ready, 1))
 
     sent = []
     arrivals = {}
@@ -145,7 +139,8 @@
         (4, lambda to: w2n_all.at[feat], lambda who: w2n_all.at[who]),
         (5, lambda to: w2s_all.at[feat], lambda who: w2s_all.at[who]),
     ]
-    for item, source, target in groups:
+
+    def exchange(item, source, target):
         for df in range(1, feats):
             to = lax.rem(feat + df, feats)
             come = lax.rem(feat + feats - df, feats)
@@ -158,6 +153,24 @@
                 source(to), target(come), a_send.at[item, df], a_recv.at[item, df], node, to
             )
 
+    for item in (2, 3, 0):
+        exchange(*groups[item])
+
+    total = None
+    for c in range(e1_chunks):
+        e1_loads[c].wait()
+        term = jnp.dot(
+            feat_full[:, c * e1_rows : (c + 1) * e1_rows],
+            edge1[c].astype(jnp.bfloat16),
+            preferred_element_type=jnp.float32,
+        )
+        total = term if total is None else total + term
+    agg_own[...] = (total / FAN1).astype(jnp.bfloat16)
+    for copy in e2_loads:
+        copy.start()
+    for item in (1, 4, 5):
+        exchange(*groups[item])
+
     def contract(weight, values):
         return lax.dot_general(
             weight, values, (((0,), (0,)), ((), ())), preferred_element_type=jnp.float32
@@ -188,6 +201,8 @@
         projected = term if projected is None else projected + term
     p_all[node] = projected.astype(p_all.dtype)
 
+    pl.when(odd == 1)(functools.partial(hear, 2 * (nodes - 1)))
+    pl.when(odd == 0)(lambda: pl.semaphore_wait(ready, 1))
     p_arrive = {}
     for dn in range(1, nodes):
         to = lax.rem(node + dn, nodes)
@@ -261,6 +276,7 @@
     mine = node * feats + feat
     loss_all[mine] = loss
 
+    others = [(dn, df) for dn in range(nodes) for df in range(feats) if dn or df]
     d_arrive = []
     for index, (dn, df) in enumerate(others):
         to_node = lax.rem(node + dn, nodes)
@@ -295,7 +311,7 @@
     chunks = 4
     ndev = nodes * feats
     bf16, f32, i32 = jnp.bfloat16, jnp.float32, jnp.int32
-    anywhere = pl.BlockSpec(memory_space=pl.ANY)
+    anywhere = pl.BlockSpec(memory_space=pltpu.HBM)
     scalar = pl.BlockSpec(memory_space=pltpu.SMEM)
     sems = pltpu.SemaphoreType.DMA
     loss, mean = pl.pallas_call(
@@ -344,11 +360,11 @@
             sems((feats,)),
             sems((ndev,)),
             sems((ndev,)),
+            pltpu.SemaphoreType.REGULAR,
         ],
         compiler_params=pltpu.CompilerParams(
             collective_id=0,
             has_side_effects=True,
-            vmem_limit_bytes=40 * 1024 * 1024,
         ),
     )(
         features,

time: 41.3 us -> 32.1 us (0.78)
  local copies, waits for them, and re-layouts: 8.46 us -> 1.26 us
  Pallas kernels: 29.9 us -> 28.2 us
    unnamed x19 -> x1, local copies, waits for them, and re-layouts: 8.46 us -> 1.26 us
    pallas_call x1, Pallas kernels: 29.9 us -> 28.2 us  [local(): pl.pallas_call(functools.partial(kernel, nodes, feats), out_shape=(jax.Sh...]
where the time goes in v2:
time: 32.1 us; the launch traced here: 31.9 us
  Pallas kernels  28.2 us (88%)
  between operations  2.41 us (8%)
  local copies, waits for them, and re-layouts  1.26 us (4%)
    pallas_call x1, Pallas kernels, local(): pl.pallas_call(functools.partial(kernel, nodes, feats), out_shape=(jax.Sh...  28.2 us
    unnamed x1, local copies, waits for them, and re-layouts  1.26 us

profile of v2, /device:TPU:0, one launch (start us, length us, event | category | flops | bytes accessed | tf_op | source)
XLA Modules:
  0.0 31.9 jit_solution(4933484069928380325)
XLA Ops:
  0.6 28.2 %shard_map.113 = (f32[1,1024]{1,0:T(1,128)}, f32[1,1]{1,0:T(1,128)}) custom-call(bf16[25,1024]{1,0:T(8,128)(2,1)} %features.1, s32[1024,1024]{1,0:T(8,128)} %edges_one.1, bf16[25,256]{1,0:T(8,128)(2,1)} %w1_self.1, bf16[25,256]{1,0:T(8,128)(2,1)} %w1_nbr.1, s32[1,4]{1,0:T(1,128)} %need.1, s32[1,4]{1,0:T(1,128)} %live.1, s32[4096,1024]{1,0:T(8,128)} %edges_two.1, ...), custom_call_target="tpu_custom_call" | custom-call | tf_op jit(solution)/shard_map/pallas_call | solution.py:317
  28.9 1.3 %copy.14 = f32[1024]{0:T(1024)} copy(f32[1024]{0:T(1024)} %bitcast.8) | data formatting | bytes 8192

commit v3 on v2

--- a/solution.py
+++ b/solution.py
@@ -203,8 +203,9 @@
 
     pl.when(odd == 1)(functools.partial(hear, 2 * (nodes - 1)))
     pl.when(odd == 0)(lambda: pl.semaphore_wait(ready, 1))
+    half = nodes // 2
     p_arrive = {}
-    for dn in range(1, nodes):
+    for dn in sorted(range(1, nodes), key=lambda d: abs(d - half)):
         to = lax.rem(node + dn, nodes)
         come = lax.rem(node + nodes - dn, nodes)
         copy = remote(p_all.at[node], p_all.at[node], p_send.at[dn], p_recv.at[dn], to, feat)
@@ -232,7 +233,6 @@
 
     e2_loads[0].wait()
     gathered = gather(0, p_all[node])
-    half = nodes // 2
     e2_loads[2].wait()
     p_arrive[1].wait_recv()
     gathered = gathered + gather(2, p_all[lax.rem(node + nodes - 1, nodes)])
@@ -308,7 +308,7 @@
     share, classes = w2_self.shape
     quarter = block // feats
     slots = need.shape[1]
-    chunks = 4
+    chunks = 2
     ndev = nodes * feats
     bf16, f32, i32 = jnp.bfloat16, jnp.float32, jnp.int32
     anywhere = pl.BlockSpec(memory_space=pltpu.HBM)

time: 32.1 us -> 31.5 us (0.981)
  Pallas kernels: 28.2 us -> 27.6 us
    pallas_call x1, Pallas kernels: 28.2 us -> 27.6 us  [local(): pl.pallas_call(functools.partial(kernel, nodes, feats), out_shape=(jax.Sh...]
where the time goes in v3:
time: 31.5 us; the launch traced here: 31.3 us
  Pallas kernels  27.6 us (88%)
  between operations  2.41 us (8%)
  local copies, waits for them, and re-layouts  1.26 us (4%)
    pallas_call x1, Pallas kernels, local(): pl.pallas_call(functools.partial(kernel, nodes, feats), out_shape=(jax.Sh...  27.6 us
    unnamed x1, local copies, waits for them, and re-layouts  1.26 us

profile of v3, /device:TPU:0, one launch (start us, length us, event | category | flops | bytes accessed | tf_op | source)
XLA Modules:
  0.0 31.3 jit_solution(13325377624532005600)
XLA Ops:
  0.6 27.6 %shard_map.113 = (f32[1,1024]{1,0:T(1,128)}, f32[1,1]{1,0:T(1,128)}) custom-call(bf16[25,1024]{1,0:T(8,128)(2,1)} %features.1, s32[1024,1024]{1,0:T(8,128)} %edges_one.1, bf16[25,256]{1,0:T(8,128)(2,1)} %w1_self.1, bf16[25,256]{1,0:T(8,128)(2,1)} %w1_nbr.1, s32[1,4]{1,0:T(1,128)} %need.1, s32[1,4]{1,0:T(1,128)} %live.1, s32[4096,1024]{1,0:T(8,128)} %edges_two.1, ...), custom_call_target="tpu_custom_call" | custom-call | tf_op jit(solution)/shard_map/pallas_call | solution.py:317
  28.3 1.3 %copy.14 = f32[1024]{0:T(1024)} copy(f32[1024]{0:T(1024)} %bitcast.8) | data formatting | bytes 8192
